TPU v7x, 512 devices: a whole 4x4x16 slice. The times are simulated.
512 devices in a mesh: batch: 64 (over y, z), table: 8 (over x, core).
Axes of the slice: x: 4, y: 4, z: 16, core: 2. Of those that a mesh axis runs over, the one named last changes fastest.
Arguments:
- embeddings: bfloat16 [64, 2048, 128], P('table'), may hold values from -0.59765625 to 0.59765625
- feature_ids: int32 [65536, 512], P('batch', 'table'), may hold values from 0 to 2047
- counts: int32 [65536, 64], P('batch', 'table'), may hold values from 0 to 8, as said below
Outputs:
- gram: bfloat16 [65536, 4096], P(('batch', 'table'))
- offsets: int32 [65536], P(('batch', 'table'))
Inputs may be any that keep to these rules, and one draw needn't show every extreme that they name: `counts`: the value 8 occurs in every device's block.
All inputs are finite; a program needn't handle non-finite values.
Results may differ from a plain program's by a relative error of at most 0.001.
The roundings to bfloat16 on the way count: a program that leaves them out, or rounds other values in their place, can miss the bound.
Values may be sent and summed in bfloat16 or wider, within the bound.
A program may use at most 64 MiB of HBM per device.

v0:
```python
import jax
import jax.numpy as jnp
from jax import lax
from jax.sharding import Mesh
from jax.sharding import PartitionSpec as P

MAXF = 8
TABLE = ("table_0", "table_1")
BATCH_TABLE = ("batch_0", "batch_1", "table_0", "table_1")
BATCH = ("batch_0", "batch_1")


def cut_along(shard, dim, count):
    before, after = (shard.shape[:dim], shard.shape[dim + 1 :])
    return jnp.moveaxis(shard.reshape(*before, count, -1, *after), dim, 0)


def edges_of(length, count):
    unit = 8 if length >= 8 * count else 1
    return [length // unit * k // count * unit for k in range(1, count)]


def in_order(tiles, dim):
    shape = list(tiles.shape[1:])
    shape[dim] *= tiles.shape[0]
    return jnp.moveaxis(tiles, 0, dim).reshape(shape)


def several_exchanges(shard, axis, pieces, split_dim, concat_dim):
    tiles = cut_along(shard, split_dim, lax.axis_size(axis))
    split_at = max(range(1, max(2, tiles.ndim - 1)), key=lambda d: tiles.shape[d])
    done = []
    for piece in jnp.split(tiles, edges_of(tiles.shape[split_at], pieces), axis=split_at):
        if piece.size:
            done.append(lax.all_to_all(piece, axis, split_axis=0, concat_axis=0, tiled=True))
    return in_order(jnp.concatenate(done, axis=split_at), concat_dim)


def filled_with(shard, identity):
    return jnp.broadcast_to(jnp.asarray(identity, shard.dtype), shard.shape)


def entering(shard, axes, combine, identity):
    before = start = filled_with(shard, identity)
    subtotal = shard
    for axis in reversed(axes):
        count, here = (lax.axis_size(axis), lax.axis_index(axis))
        pieces = lax.all_gather(subtotal, axis)
        inside, subtotal = (start, start)
        for k in range(count):
            passed = k < here
            subtotal = combine(subtotal, pieces[k])
            inside = jnp.where(passed, subtotal, inside)
        before = combine(inside, before)
    return before


def pool_one(table, idents, number):
    entries = table.shape[0]
    column = jnp.arange(entries, dtype=jnp.int32)[None, :]
    weights = jnp.zeros((idents.shape[0], entries), jnp.float32)
    for slot in range(idents.shape[1]):
        alive = (number > slot)[:, None]
        match = jnp.logical_and(idents[:, slot][:, None] == column, alive)
        weights = weights + match.astype(jnp.float32)
    return jnp.dot(weights.astype(jnp.bfloat16), table, preferred_element_type=jnp.float32)


def body(embeddings, feature_ids, counts):
    local = embeddings.shape[0]
    rows = feature_ids.shape[0]
    idents = feature_ids.reshape(rows, local, MAXF).transpose(1, 0, 2)
    pooled = lax.map(lambda a: pool_one(a[0], a[1], a[2]), (embeddings, idents, counts.T))
    pooled = pooled.transpose(1, 0, 2).astype(jnp.bfloat16)
    gotten, got_counts = (
        several_exchanges(pooled, TABLE, 2, 0, 1),
        several_exchanges(counts, TABLE, 2, 0, 1),
    )
    samples = gotten.shape[0]
    gram = jnp.einsum("sie,sje->sij", gotten, gotten, preferred_element_type=jnp.float32)
    gram = gram.astype(jnp.bfloat16).reshape(samples, -1)
    live = jnp.sum((got_counts > 0).astype(jnp.int32), axis=1)
    pairs = live * (live - 1) // 2
    within = jnp.cumsum(pairs) - pairs
    total = jnp.sum(pairs)
    earlier = entering(total, BATCH_TABLE, lambda first, later: first + later, jnp.int32(0))
    return (gram, (within + earlier).astype(jnp.int32))


def solution(mesh):
    split = Mesh(mesh.devices.reshape(4, 16, 4, 2), ("batch_0", "batch_1", "table_0", "table_1"))
    in_specs = (P(TABLE, None, None), P(BATCH, TABLE), P(BATCH, TABLE))
    out_specs = (P(BATCH_TABLE, None), P(BATCH_TABLE))
    return jax.shard_map(body, mesh=split, in_specs=in_specs, out_specs=out_specs, check_vma=False)
```

profile of v0, /device:TPU:2, one launch (start us, length us, event | category | flops | bytes accessed | tf_op | source)
XLA Modules:
  0.0 262.4 jit_solution(12264101208441681259)
XLA Ops:
  0.6 0.9 fusion.31
  2.2 9.1 %all-to-all-start.3 = ((s32[8,1,512]{2,1,0:T(1,128)}), s32[8,1,512]{2,1,0:T(1,128)S(1)}, u32[]{:S(2)}, u32[]{:S(2)}) async-start(s32[8,1,512]{2,1,0:T(1,128)} %reshape.186), calls=%async_computation.3 | async-start | bytes 32768 | tf_op jit(solution)/shard_map/all_to_all | solution.py:35
  11.4 137.0 %while.10 = (s32[]{:T(128)}, bf16[8,1024,128]{2,1,0:T(8,128)(2,1)}, s32[8,1024,8]{1,2,0:T(8,128)}, s32[8,1024]{1,0:T(8,128)}, bf16[8,2048,128]{2,1,0:T(8,128)(2,1)}, /*index=5*/s32[]{:T(128)}) while((s32[]{:T(128)}, bf16[8,1024,128]{2,1,0:T(8,128)(2,1)}, s32[8,1024,8]{1,2,0:T(8,128)}, s32[8,1024]{1,0:T(8,128)}, ...), condition=%wide.region_1.2_spmd, body=%wide.region_0.1_spmd.sunk | while | flops 603987968 | bytes 1233997 | solution.py:73
  11.4 0.8 dynamic-slice_bitcast_fusion.2
  12.1 0.9 compare_reduce_fusion.9
  13.0 15.5 %fusion.41 = bf16[8,1024,128]{2,1,0:T(8,128)(2,1)} fusion(bf16[8,1024,128]{2,1,0:T(8,128)(2,1)} %get-tuple-element.162, s32[]{:T(128)} %get-tuple-element.161, s32[1024]{0:T(1024)S(1)} %bitcast.110, s32[1024]{0:T(1024)S(1)} %bitcast.111, s32[1024]{0:T(1024)S(1)} %bitcast.112, s32[1024]{0:T(1024)S(1)} %bitcast.113, s32[1024]{0:T(1024)S(1)} %bitcast.114, ...), kind=kOutput, calls=%fused_computation.27.clone.1 | convolution fusion | flops 603979776 | bytes 1090560 | tf_op jit(solution)/shard_map/while/body/eval_jaxpr/dot_general | solution.py:66
  28.5 0.8 dynamic-slice_bitcast_fusion.2
  29.3 0.9 compare_reduce_fusion.9
  30.1 15.5 %fusion.41 = bf16[8,1024,128]{2,1,0:T(8,128)(2,1)} fusion(bf16[8,1024,128]{2,1,0:T(8,128)(2,1)} %get-tuple-element.162, s32[]{:T(128)} %get-tuple-element.161, s32[1024]{0:T(1024)S(1)} %bitcast.110, s32[1024]{0:T(1024)S(1)} %bitcast.111, s32[1024]{0:T(1024)S(1)} %bitcast.112, s32[1024]{0:T(1024)S(1)} %bitcast.113, s32[1024]{0:T(1024)S(1)} %bitcast.114, ...), kind=kOutput, calls=%fused_computation.27.clone.1 | convolution fusion | flops 603979776 | bytes 1090560 | tf_op jit(solution)/shard_map/while/body/eval_jaxpr/dot_general | solution.py:66
  45.6 0.8 dynamic-slice_bitcast_fusion.2
  46.4 0.9 compare_reduce_fusion.9
  47.3 15.4 %fusion.41 = bf16[8,1024,128]{2,1,0:T(8,128)(2,1)} fusion(bf16[8,1024,128]{2,1,0:T(8,128)(2,1)} %get-tuple-element.162, s32[]{:T(128)} %get-tuple-element.161, s32[1024]{0:T(1024)S(1)} %bitcast.110, s32[1024]{0:T(1024)S(1)} %bitcast.111, s32[1024]{0:T(1024)S(1)} %bitcast.112, s32[1024]{0:T(1024)S(1)} %bitcast.113, s32[1024]{0:T(1024)S(1)} %bitcast.114, ...), kind=kOutput, calls=%fused_computation.27.clone.1 | convolution fusion | flops 603979776 | bytes 1090560 | tf_op jit(solution)/shard_map/while/body/eval_jaxpr/dot_general | solution.py:66
  62.7 0.8 dynamic-slice_bitcast_fusion.2
  63.5 0.9 compare_reduce_fusion.9
  64.4 15.5 %fusion.41 = bf16[8,1024,128]{2,1,0:T(8,128)(2,1)} fusion(bf16[8,1024,128]{2,1,0:T(8,128)(2,1)} %get-tuple-element.162, s32[]{:T(128)} %get-tuple-element.161, s32[1024]{0:T(1024)S(1)} %bitcast.110, s32[1024]{0:T(1024)S(1)} %bitcast.111, s32[1024]{0:T(1024)S(1)} %bitcast.112, s32[1024]{0:T(1024)S(1)} %bitcast.113, s32[1024]{0:T(1024)S(1)} %bitcast.114, ...), kind=kOutput, calls=%fused_computation.27.clone.1 | convolution fusion | flops 603979776 | bytes 1090560 | tf_op jit(solution)/shard_map/while/body/eval_jaxpr/dot_general | solution.py:66
  79.8 0.8 dynamic-slice_bitcast_fusion.2
  80.6 0.9 compare_reduce_fusion.9
  81.5 15.5 %fusion.41 = bf16[8,1024,128]{2,1,0:T(8,128)(2,1)} fusion(bf16[8,1024,128]{2,1,0:T(8,128)(2,1)} %get-tuple-element.162, s32[]{:T(128)} %get-tuple-element.161, s32[1024]{0:T(1024)S(1)} %bitcast.110, s32[1024]{0:T(1024)S(1)} %bitcast.111, s32[1024]{0:T(1024)S(1)} %bitcast.112, s32[1024]{0:T(1024)S(1)} %bitcast.113, s32[1024]{0:T(1024)S(1)} %bitcast.114, ...), kind=kOutput, calls=%fused_computation.27.clone.1 | convolution fusion | flops 603979776 | bytes 1090560 | tf_op jit(solution)/shard_map/while/body/eval_jaxpr/dot_general | solution.py:66
  97.0 0.8 dynamic-slice_bitcast_fusion.2
  97.7 0.9 compare_reduce_fusion.9
  98.6 15.5 %fusion.41 = bf16[8,1024,128]{2,1,0:T(8,128)(2,1)} fusion(bf16[8,1024,128]{2,1,0:T(8,128)(2,1)} %get-tuple-element.162, s32[]{:T(128)} %get-tuple-element.161, s32[1024]{0:T(1024)S(1)} %bitcast.110, s32[1024]{0:T(1024)S(1)} %bitcast.111, s32[1024]{0:T(1024)S(1)} %bitcast.112, s32[1024]{0:T(1024)S(1)} %bitcast.113, s32[1024]{0:T(1024)S(1)} %bitcast.114, ...), kind=kOutput, calls=%fused_computation.27.clone.1 | convolution fusion | flops 603979776 | bytes 1090560 | tf_op jit(solution)/shard_map/while/body/eval_jaxpr/dot_general | solution.py:66
  114.1 0.8 dynamic-slice_bitcast_fusion.2
  114.9 0.9 compare_reduce_fusion.9
  115.7 15.5 %fusion.41 = bf16[8,1024,128]{2,1,0:T(8,128)(2,1)} fusion(bf16[8,1024,128]{2,1,0:T(8,128)(2,1)} %get-tuple-element.162, s32[]{:T(128)} %get-tuple-element.161, s32[1024]{0:T(1024)S(1)} %bitcast.110, s32[1024]{0:T(1024)S(1)} %bitcast.111, s32[1024]{0:T(1024)S(1)} %bitcast.112, s32[1024]{0:T(1024)S(1)} %bitcast.113, s32[1024]{0:T(1024)S(1)} %bitcast.114, ...), kind=kOutput, calls=%fused_computation.27.clone.1 | convolution fusion | flops 603979776 | bytes 1090560 | tf_op jit(solution)/shard_map/while/body/eval_jaxpr/dot_general | solution.py:66
  131.2 0.8 dynamic-slice_bitcast_fusion.2
  132.0 0.9 compare_reduce_fusion.9
  132.9 15.5 %fusion.41 = bf16[8,1024,128]{2,1,0:T(8,128)(2,1)} fusion(bf16[8,1024,128]{2,1,0:T(8,128)(2,1)} %get-tuple-element.162, s32[]{:T(128)} %get-tuple-element.161, s32[1024]{0:T(1024)S(1)} %bitcast.110, s32[1024]{0:T(1024)S(1)} %bitcast.111, s32[1024]{0:T(1024)S(1)} %bitcast.112, s32[1024]{0:T(1024)S(1)} %bitcast.113, s32[1024]{0:T(1024)S(1)} %bitcast.114, ...), kind=kOutput, calls=%fused_computation.27.clone.1 | convolution fusion | flops 603979776 | bytes 1090560 | tf_op jit(solution)/shard_map/while/body/eval_jaxpr/dot_general | solution.py:66
  149.0 2.9 %copy.13 = bf16[1024,8,128]{2,1,0:T(8,128)(2,1)S(1)} copy(bf16[1024,8,128]{2,0,1:T(8,128)(2,1)} %bitcast.102) | data formatting | bytes 4194304 | tf_op jit(solution)/shard_map/convert_element_type | solution.py:74
  152.0 4.8 %all-to-all-start.2 = ((s32[8,1,512]{2,1,0:T(1,128)}), s32[8,1,512]{2,1,0:T(1,128)S(1)}, u32[]{:S(2)}, u32[]{:S(2)}) async-start(s32[8,1,512]{2,1,0:T(1,128)} %reshape.188), calls=%async_computation.2 | async-start | bytes 32768 | tf_op jit(solution)/shard_map/all_to_all | solution.py:35
  156.8 1.5 fusion.30
  158.3 2.4 all-to-all-done.2
  160.7 4.9 %all-to-all-start = ((bf16[8,64,8,128]{3,2,1,0:T(8,128)(2,1)}), bf16[8,64,8,128]{3,2,1,0:T(8,128)(2,1)S(1)}, u32[]{:S(2)}, u32[]{:S(2)}) async-start(bf16[8,64,8,128]{3,2,1,0:T(8,128)(2,1)} %get-tuple-element.62), calls=%async_computation | async-start | bytes 2097152 | tf_op jit(solution)/shard_map/all_to_all | solution.py:35
  165.6 1.3 dynamic-slice
  166.9 1.3 dynamic-slice.1
  168.2 1.2 dynamic-slice.2
  171.6 8.6 %all-to-all-done = bf16[8,64,8,128]{3,2,1,0:T(8,128)(2,1)S(1)} async-done(((bf16[8,64,8,128]{3,2,1,0:T(8,128)(2,1)}), bf16[8,64,8,128]{3,2,1,0:T(8,128)(2,1)S(1)}, u32[]{:S(2)}, u32[]{:S(2)}) %all-to-all-start) | async-done | bytes 1048608 | tf_op jit(solution)/shard_map/all_to_all | solution.py:35
  180.1 5.6 %all-to-all-start.1 = ((bf16[8,64,8,128]{3,2,1,0:T(8,128)(2,1)}), bf16[8,64,8,128]{3,2,1,0:T(8,128)(2,1)}, u32[]{:S(2)}, u32[]{:S(2)}) async-start(bf16[8,64,8,128]{3,2,1,0:T(8,128)(2,1)} %get-tuple-element.63), calls=%async_computation.1 | async-start | bytes 2097152 | tf_op jit(solution)/shard_map/all_to_all | solution.py:35
  186.3 1.4 dynamic-update-slice
  187.7 1.8 all-reduce
  192.1 1.3 dynamic-slice.3
  193.4 9.3 %all-reduce.1 = s32[4]{0:T(128)S(1)} all-reduce(s32[4]{0:T(128)S(1)} %dynamic-update-slice.1), channel_id=1, replica_groups=mesh['batch_0'=4,'batch_1'=16,'table_0'=4,'table_1'=2] {'table_0'}, use_global_device_ids=true, to_apply=%add.1 | all-reduce | flops 4 | bytes 32
  206.5 22.4 %all-reduce.2 = s32[16]{0:T(128)S(1)} all-reduce(s32[16]{0:T(128)S(1)} %dynamic-update-slice.2), channel_id=1, replica_groups=mesh['batch_0'=4,'batch_1'=16,'table_0'=4,'table_1'=2] {'batch_1'}, use_global_device_ids=true, to_apply=%add.2 | all-reduce | flops 16 | bytes 128
  228.9 0.7 fusion.33
  239.6 0.7 dynamic-update-slice.3
  240.3 9.0 %all-reduce.3 = s32[4]{0:T(128)S(1)} all-reduce(s32[4]{0:T(128)S(1)} %dynamic-update-slice.3), channel_id=1, replica_groups=mesh['batch_0'=4,'batch_1'=16,'table_0'=4,'table_1'=2] {'batch_0'}, use_global_device_ids=true, to_apply=%add.3 | all-reduce | flops 4 | bytes 32
  256.0 2.9 %fusion.25 = bf16[128,64,64]{2,1,0:T(8,128)(2,1)S(1)} fusion(bf16[8,64,8,128]{3,2,1,0:T(8,128)(2,1)} %all-to-all-done.1, bf16[8,64,8,128]{3,2,1,0:T(8,128)(2,1)S(1)} %all-to-all-done), kind=kOutput, calls=%fused_computation.46 | convolution fusion | flops 135790592 | bytes 3145728 | tf_op jit(solution)/shard_map/sie,sje->sij/dot_general | solution.py:80
  258.9 2.2 copy.15
  261.1 1.3 copy.17
  (34 shorter events, 8.5 us)
Async XLA Ops:
  2.2 149.7 %all-to-all-start.3 = ((s32[8,1,512]{2,1,0:T(1,128)}), s32[8,1,512]{2,1,0:T(1,128)S(1)}, u32[]{:S(2)}, u32[]{:S(2)}) async-start(s32[8,1,512]{2,1,0:T(1,128)} %reshape.186), calls=%async_computation.3 | async-start | bytes 32768 | tf_op jit(solution)/shard_map/all_to_all | solution.py:35
  152.0 8.7 %all-to-all-start.2 = ((s32[8,1,512]{2,1,0:T(1,128)}), s32[8,1,512]{2,1,0:T(1,128)S(1)}, u32[]{:S(2)}, u32[]{:S(2)}) async-start(s32[8,1,512]{2,1,0:T(1,128)} %reshape.188), calls=%async_computation.2 | async-start | bytes 32768 | tf_op jit(solution)/shard_map/all_to_all | solution.py:35
  160.7 19.4 %all-to-all-start = ((bf16[8,64,8,128]{3,2,1,0:T(8,128)(2,1)}), bf16[8,64,8,128]{3,2,1,0:T(8,128)(2,1)S(1)}, u32[]{:S(2)}, u32[]{:S(2)}) async-start(bf16[8,64,8,128]{3,2,1,0:T(8,128)(2,1)} %get-tuple-element.62), calls=%async_computation | async-start | bytes 2097152 | tf_op jit(solution)/shard_map/all_to_all | solution.py:35
  180.1 75.8 %all-to-all-start.1 = ((bf16[8,64,8,128]{3,2,1,0:T(8,128)(2,1)}), bf16[8,64,8,128]{3,2,1,0:T(8,128)(2,1)}, u32[]{:S(2)}, u32[]{:S(2)}) async-start(bf16[8,64,8,128]{3,2,1,0:T(8,128)(2,1)} %get-tuple-element.63), calls=%async_computation.1 | async-start | bytes 2097152 | tf_op jit(solution)/shard_map/all_to_all | solution.py:35
where the time goes:
time: 265 us; the launch traced here: 262 us
  matrix products  127 us (48%)
  blocking collectives  42.6 us (16%)
  local copies, waits for them, and re-layouts  28.4 us (11%)
  starting transfers between devices  24.4 us (9%)
  between operations  19.5 us (7%)
  waiting for transfers between devices  11 us (4%)
  other arithmetic  9.86 us (4%)
    dot_general x8, matrix products, pool_one(): jnp.dot(weights.astype(jnp.bfloat16), table, preferred_element_type=jnp.f...  124 us
    unnamed x4, blocking collectives  42.6 us
    all_to_all x4, starting transfers between devices, several_exchanges(): lax.all_to_all(piece, axis, split_axis=0, concat_axis=0, tiled=True)  24.4 us
    unnamed x17, local copies, waits for them, and re-layouts  11.4 us
    all_to_all x4, waiting for transfers between devices, several_exchanges(): lax.all_to_all(piece, axis, split_axis=0, concat_axis=0, tiled=True)  11 us
    gt x8, other arithmetic, pool_one(): alive = (number > slot)[:, None]  6.95 us
    squeeze x8, local copies, waits for them, and re-layouts, body(): lax.map(lambda a: pool_one(a[0], a[1], a[2]), (embeddings, idents, counts...  6.08 us
  transfers between devices with their start and end apart: 4, of which 2 were waited for; matrix products, arithmetic and copies ran while one was open for 60% of the time, Pallas kernels for 0%

commit v1 on v0

v1 whole, which is shorter than its diff:
```python
import jax
import jax.numpy as jnp
from jax import lax
from jax.experimental import pallas as pl
from jax.experimental.pallas import tpu as pltpu
from jax.sharding import PartitionSpec as P

BF = jnp.bfloat16
F32 = jnp.float32
I32 = jnp.int32
MESH = pl.DeviceIdType.MESH
MAXF = 8
NT = 8
NK = 8
NY, NZ = 4, 16
LANES = 128
TRI = (((1,), (1,)), ((), ()))


def make_keys(ids, cnt, ka, kb):
    lane = lax.broadcasted_iota(I32, (8, LANES), 1)
    sub = lax.broadcasted_iota(I32, (8, LANES), 0)
    place = [jnp.logical_and((sub & 3) == b, (lane >> 5) == b) for b in range(4)]

    def tile(q, carry):
        c0 = pl.multiple_of(q * LANES, LANES)
        for t in range(NT):
            v = ids[t * 8 : t * 8 + 8, pl.ds(c0, LANES)]
            v = jnp.where(sub >= cnt[t : t + 1, pl.ds(c0, LANES)], 2048, v)
            turned = [v] + [pltpu.roll(v, 32 * k, 1) for k in range(1, 4)]
            for a in range(4):
                m = jnp.zeros_like(v)
                for b in range(4):
                    m = jnp.where(place[b], turned[(b - a) % 4], m)
                m = m + pltpu.roll(m, 7, 0)
                m = m + pltpu.roll(m, 6, 0)
                za = (((m >> 8) << 5) + (lane & 31)).astype(F32)
                zb = (m & 255).astype(F32)
                for h in range(2):
                    ka[q, t, a : a + 1, h * 128 : h * 128 + 128] = za[4 * h : 4 * h + 1, :]
                    kb[q, t, a : a + 1, h * 128 : h * 128 + 128] = zb[4 * h : 4 * h + 1, :]
        return carry

    lax.fori_loop(0, 8, tile, 0)


def pool_body(ids, cnt, tab_hbm, out, offs, tab, ka, kb, iota, w, stage, sb, lv, lvall, tot, ztot, yline,
              tsem, ssem, rsem, lsem, lss, lrs, zss, zrs, yss, yrs):
    b, k = lax.axis_index("batch"), lax.axis_index("table")
    y, z = b // NZ, b % NZ
    x, c = k // 2, k % 2

    bar = pltpu.get_barrier_semaphore()
    for d in range(1, NK):
        pl.semaphore_signal(bar, inc=1, device_id=(b, (k + d) % NK), device_id_type=MESH)
    for d in range(1, NZ):
        pl.semaphore_signal(bar, inc=1, device_id=(y * NZ + (z + d) % NZ, k), device_id_type=MESH)
    for d in range(1, NY):
        pl.semaphore_signal(bar, inc=1, device_id=(((y + d) % NY) * NZ + z, k), device_id_type=MESH)

    def table_copy(t):
        return pltpu.make_async_copy(tab_hbm.at[t], tab.at[t], tsem.at[t])

    for t in range(NT):
        table_copy(t).start()

    iota[...] = lax.broadcasted_iota(I32, (256, 256), 0).astype(F32).astype(BF)
    make_keys(ids, cnt, ka, kb)

    for q in range(8):
        on = (cnt[:, q * 128 : q * 128 + 128] > 0).astype(I32)
        lv[q : q + 1, :] = jnp.sum(on, axis=0, keepdims=True)

    def turn(j):
        return (2 + 3 * j + 3 * ((j * (j - 1)) // 2)) % 4

    def chunk_copy(j, cc):
        h, xd = j // 4, (x + turn(j % 4)) % 4
        return pltpu.make_async_remote_copy(
            src_ref=sb.at[j, cc], dst_ref=out.at[h, k], send_sem=ssem.at[j * 2 + cc],
            recv_sem=rsem.at[k * 2 + h], device_id=(b, xd * 2 + cc), device_id_type=MESH)

    def partner_copy(j):
        h = j // 4
        return pltpu.make_async_remote_copy(
            src_ref=sb.at[j, 1 - c], dst_ref=out.at[h, k], send_sem=ssem.at[j * 2],
            recv_sem=rsem.at[k * 2 + h], device_id=(b, x * 2 + 1 - c), device_id_type=MESH)

    def own_copy(j):
        h = j // 4
        return pltpu.make_async_copy(sb.at[j, c], out.at[h, k], lsem.at[h])

    def live_copy(d):
        return pltpu.make_async_remote_copy(
            src_ref=lv, dst_ref=lvall.at[k], send_sem=lss.at[d], recv_sem=lrs.at[k],
            device_id=(b, (k + d) % NK), device_id_type=MESH)

    def z_copy(d):
        return pltpu.make_async_remote_copy(
            src_ref=tot, dst_ref=ztot.at[z], send_sem=zss.at[d], recv_sem=zrs.at[z],
            device_id=(y * NZ + (z + d) % NZ, k), device_id_type=MESH)

    def y_copy(d):
        return pltpu.make_async_remote_copy(
            src_ref=yline.at[y], dst_ref=yline.at[y], send_sem=yss.at[d], recv_sem=yrs.at[y],
            device_id=(((y + d) % NY) * NZ + z, k), device_id_type=MESH)

    def arrival(ref, sem):
        return pltpu.make_async_remote_copy(
            src_ref=ref, dst_ref=ref, send_sem=sem, recv_sem=sem, device_id=(b, k), device_id_type=MESH)

    def rows_of(i):
        j = i // 4
        return j, j // 4, (x + turn(j % 4)) % 4, (i % 4) * 2

    def first(i, slot):
        j, h, xd, t0 = rows_of(i)
        one, zero = jnp.ones((16, 256), BF), jnp.zeros((16, 256), BF)
        for tt in range(2):
            for g in range(4):
                q, a = xd * 2 + g // 2, h * 2 + g % 2
                ra = jnp.broadcast_to(ka[q, t0 + tt, pl.ds(a, 1), :], (16, 256)).astype(BF)
                rb = jnp.broadcast_to(kb[q, t0 + tt, pl.ds(a, 1), :], (16, 256)).astype(BF)
                la, lb = [], []
                for r in range(16):
                    row = iota[r * 16 : r * 16 + 16, :]
                    la.append(jnp.where(row == ra, one, zero))
                    lb.append(jnp.where(row == rb, one, zero))
                n = lax.dot_general(jnp.concatenate(la, 0), jnp.concatenate(lb, 0), TRI,
                                    preferred_element_type=F32).astype(BF)
                for hi in range(8):
                    w[slot, tt, hi, g * 32 : g * 32 + 32, :] = n[hi * 32 : hi * 32 + 32, :]

    def second(i, slot):
        j, h, xd, t0 = rows_of(i)
        for tt in range(2):
            acc = None
            for hi in range(8):
                d = jnp.dot(w[slot, tt, hi], tab[t0 + tt, hi * 256 : hi * 256 + 256, :],
                            preferred_element_type=F32)
                acc = d if acc is None else acc + d
            stage[pl.ds(t0 + tt, 128, 8), :] = acc

    def finish(j):
        for cc in range(2):
            sb[j, cc] = stage[cc * 512 : cc * 512 + 512, :].astype(BF)

        @pl.when(j % 4 < 3)
        def _():
            for cc in range(2):
                chunk_copy(j, cc).start()

        @pl.when(j % 4 == 3)
        def _():
            partner_copy(j).start()
            own_copy(j).start()

    def pairs_of():
        live = lv[...]
        for d in range(1, NK):
            live = live + lvall[(k + d) % NK]
        return (live * (live - 1)) >> 1

    def sum_all(v):
        s = jnp.sum(jnp.sum(v, axis=0, keepdims=True), axis=1, keepdims=True)
        return jnp.broadcast_to(s, (8, LANES))

    def step(i, carry):
        slot = i % 2

        @pl.when(i <= 4)
        def _():
            table_copy((i - 1) * 2).wait()
            table_copy((i - 1) * 2 + 1).wait()

        second(i - 1, 1 - slot)
        first(i, slot)

        @pl.when(i == 4)
        def _():
            pl.semaphore_wait(bar, NK - 1 + NZ - 1 + NY - 1)
            for d in range(1, NK):
                live_copy(d).start()

        @pl.when(i % 4 == 0)
        def _():
            finish(i // 4 - 1)

        @pl.when(i == 9)
        def _():
            for d in range(1, NK):
                arrival(lvall.at[(k + d) % NK], lrs.at[(k + d) % NK]).wait_recv()
            tot[...] = sum_all(pairs_of())
            ztot[z] = tot[...]
            for d in range(1, NZ):
                z_copy(d).start()

        @pl.when(i == 21)
        def _():
            for d in range(1, NZ):
                arrival(ztot.at[(z + d) % NZ], zrs.at[(z + d) % NZ]).wait_recv()
            line = ztot[0]
            for d in range(1, NZ):
                line = line + ztot[d]
            yline[y] = line
            for d in range(1, NY):
                y_copy(d).start()

        return carry

    first(0, 0)
    lax.fori_loop(1, 32, step, 0)
    second(31, 1)
    finish(7)

    for d in range(1, NY):
        arrival(yline.at[(y + d) % NY], yrs.at[(y + d) % NY]).wait_recv()
    lane = lax.broadcasted_iota(I32, (8, LANES), 1)
    sub = lax.broadcasted_iota(I32, (8, LANES), 0)
    before = jnp.zeros((8, LANES), I32)
    for d in range(NY):
        before = before + jnp.where(d < y, yline[d], 0)
    for d in range(NZ):
        before = before + jnp.where(d < z, ztot[d], 0)
    pairs = pairs_of()
    run = pairs
    for n in range(7):
        run = run + jnp.where(lane >= (1 << n), pltpu.roll(run, 1 << n, 1), 0)
    before = before + sum_all(jnp.where(sub < k, pairs, 0))
    mine = jnp.sum(jnp.where(sub == k, run - pairs, 0), axis=0, keepdims=True)
    offs[...] = mine + before[0:1, :]

    for d in range(1, NK):
        live_copy(d).wait_send()
    for d in range(1, NZ):
        z_copy(d).wait_send()
    for d in range(1, NY):
        y_copy(d).wait_send()
    for h in range(2):
        for j in range(3):
            for cc in range(2):
                chunk_copy(h * 4 + j, cc).wait_send()
        partner_copy(h * 4 + 3).wait_send()
        own_copy(h * 4 + 3).wait()
        for d in range(1, NK):
            src = (k + d) % NK
            arrival(out.at[h, src], rsem.at[src * 2 + h]).wait_recv()


def pool_exchange(ids, cnt, tab):
    dma = pltpu.SemaphoreType.DMA
    return pl.pallas_call(
        pool_body,
        out_shape=(jax.ShapeDtypeStruct((2, NK, 512, LANES), BF), jax.ShapeDtypeStruct((1, LANES), I32)),
        in_specs=[pl.BlockSpec(memory_space=pltpu.VMEM)] * 2 + [pl.BlockSpec(memory_space=pl.ANY)],
        out_specs=(pl.BlockSpec(memory_space=pl.ANY), pl.BlockSpec(memory_space=pltpu.VMEM)),
        scratch_shapes=[
            pltpu.VMEM((NT, 2048, LANES), BF),
            pltpu.VMEM((8, NT, 4, 256), F32),
            pltpu.VMEM((8, NT, 4, 256), F32),
            pltpu.VMEM((256, 256), BF),
            pltpu.VMEM((2, 2, 8, 128, 256), BF),
            pltpu.VMEM((1024, LANES), F32),
            pltpu.VMEM((8, 2, 512, LANES), BF),
            pltpu.VMEM((8, LANES), I32),
            pltpu.VMEM((NK, 8, LANES), I32),
            pltpu.VMEM((8, LANES), I32),
            pltpu.VMEM((NZ, 8, LANES), I32),
            pltpu.VMEM((NY, 8, LANES), I32),
            dma((NT,)), dma((16,)), dma((16,)), dma((2,)),
            dma((NK,)), dma((NK,)), dma((NZ,)), dma((NZ,)), dma((NY,)), dma((NY,)),
        ],
        compiler_params=pltpu.CompilerParams(
            collective_id=0, has_side_effects=True, vmem_limit_bytes=40 * 2**20),
        name="pool_exchange",
    )(ids, cnt, tab)


def gram_body(src, out, g):
    low = lax.broadcasted_iota(I32, (16, LANES), 1) < 64
    for half in range(2):
        for p in range(8):
            r0 = half * 128 + p * 16
            got = [src[0, s, r0 : r0 + 16, :].astype(F32) for s in range(NK)]
            even = jnp.concatenate([v[0:8] for v in got], 0).astype(BF)
            odd = jnp.concatenate([v[8:16] for v in got], 0).astype(BF)
            for n, m in ((0, even), (1, odd)):
                full = lax.dot_general(m, jnp.concatenate([m, m], 0), TRI, preferred_element_type=F32)
                g[half, (p * 2 + n) * 64 : (p * 2 + n) * 64 + 64, :] = full
    for half in range(2):
        for i in range(32):
            lo = g[half, pl.ds(2 * i, 16, 64), :]
            hi = g[half, pl.ds(2 * i + 1, 16, 64), :]
            out[half * 16 : half * 16 + 16, i * 128 : i * 128 + 128] = jnp.where(low, lo, hi).astype(BF)


def gram(got):
    return pl.pallas_call(
        gram_body,
        grid=(4,),
        out_shape=jax.ShapeDtypeStruct((128, 4096), BF),
        in_specs=[pl.BlockSpec((1, NK, 256, LANES), lambda i: (i // 2, 0, i % 2, 0))],
        out_specs=pl.BlockSpec((32, 4096), lambda i: (i, 0)),
        scratch_shapes=[pltpu.VMEM((2, 1024, LANES), F32)],
        name="gram",
    )(got)


def body(embeddings, feature_ids, counts):
    got, offsets = pool_exchange(feature_ids.T, counts.T, embeddings)
    return gram(got), offsets.reshape(LANES)


def solution(mesh):
    return jax.shard_map(
        body, mesh=mesh,
        in_specs=(P("table", None, None), P("batch", "table"), P("batch", "table")),
        out_specs=(P(("batch", "table"), None), P(("batch", "table"))),
        check_vma=False)
```

time: 265 us -> 58.3 us (0.22)
  the two profiles are of different devices: /device:TPU:2 before, /device:TPU:1 now
where the time goes in v1:
time: 58.3 us; the launch traced here: 58 us
  Pallas kernels  51.7 us (89%)
  local copies, waits for them, and re-layouts  5.72 us (10%)
  between operations  0.66 us (1%)
    pallas_call x1, Pallas kernels, pool_exchange(): pl.pallas_call(pool_body, out_shape=(jax.ShapeDtypeStruct((2, NK, 512, LA...  45.2 us
    pallas_call x1, Pallas kernels, gram(): pl.pallas_call(gram_body, grid=(4,), out_shape=jax.ShapeDtypeStruct((128,...  6.43 us
    unnamed x9, local copies, waits for them, and re-layouts  5.72 us

profile of v1, /device:TPU:1, one launch (start us, length us, event | category | flops | bytes accessed | tf_op | source)
XLA Modules:
  0.0 58.0 jit_solution(5427866288142411071)
XLA Ops:
  0.6 0.0 copy-start
  0.6 2.2 %copy-done = bf16[8,2048,128]{2,1,0:T(8,128)(2,1)S(1)} copy-done((bf16[8,2048,128]{2,1,0:T(8,128)(2,1)S(1)}, bf16[8,2048,128]{2,1,0:T(8,128)(2,1)}, u32[]{:S(2)}) %copy-start) | copy-done | bytes 4194328
  2.8 0.0 copy-start.2
  2.8 0.9 %copy-done.2 = s32[1024,64]{0,1:T(8,128)S(1)} copy-done((s32[1024,64]{0,1:T(8,128)S(1)}, s32[1024,64]{0,1:T(8,128)}, u32[]{:S(2)}) %copy-start.2) | copy-done | bytes 262168
  3.8 0.0 copy-start.3
  3.8 0.8 %copy-done.3 = s32[1024,8]{0,1:T(8,128)S(1)} copy-done((s32[1024,8]{0,1:T(8,128)S(1)}, s32[1024,8]{0,1:T(8,128)}, u32[]{:S(2)}) %copy-start.3) | copy-done | bytes 32792
  4.5 45.2 %pool_exchange.1 = (bf16[2,8,512,128]{3,2,1,0:T(8,128)(2,1)S(1)}, s32[1,128]{1,0:T(1,128)S(1)}) custom-call(s32[64,1024]{1,0:T(8,128)S(1)} %bitcast.3, s32[8,1024]{1,0:T(8,128)S(1)} %bitcast.4, bf16[8,2048,128]{2,1,0:T(8,128)(2,1)S(1)} %copy-done), custom_call_target="tpu_custom_call" | custom-call | tf_op jit(solution)/shard_map/pool_exchange/pallas_call | solution.py:252
  49.8 0.0 copy-start.1
  49.8 1.3 %copy-done.1 = bf16[2,8,512,128]{3,2,1,0:T(8,128)(2,1)} copy-done((bf16[2,8,512,128]{3,2,1,0:T(8,128)(2,1)}, bf16[2,8,512,128]{3,2,1,0:T(8,128)(2,1)S(1)}, u32[]{:S(2)}) %copy-start.1) | copy-done | bytes 2097176
  51.1 6.4 %gram.1 = bf16[128,4096]{1,0:T(8,128)(2,1)} custom-call(bf16[2,8,512,128]{3,2,1,0:T(8,128)(2,1)} %copy-done.1), custom_call_target="tpu_custom_call" | custom-call | tf_op jit(solution)/shard_map/gram/pallas_call | solution.py:298
  57.5 0.5 copy.6
Async XLA Ops:
  0.6 2.2 %copy-start = (bf16[8,2048,128]{2,1,0:T(8,128)(2,1)S(1)}, bf16[8,2048,128]{2,1,0:T(8,128)(2,1)}, u32[]{:S(2)}) copy-start(bf16[8,2048,128]{2,1,0:T(8,128)(2,1)} %tab_hbm.1) | copy-start | bytes 12582916
  2.8 0.9 %copy-start.2 = (s32[1024,64]{0,1:T(8,128)S(1)}, s32[1024,64]{0,1:T(8,128)}, u32[]{:S(2)}) copy-start(s32[1024,64]{0,1:T(8,128)} %param.4) | copy-start | bytes 786436
  3.8 0.8 %copy-start.3 = (s32[1024,8]{0,1:T(8,128)S(1)}, s32[1024,8]{0,1:T(8,128)}, u32[]{:S(2)}) copy-start(s32[1024,8]{0,1:T(8,128)} %param.5) | copy-start | bytes 98308
  49.8 1.3 %copy-start.1 = (bf16[2,8,512,128]{3,2,1,0:T(8,128)(2,1)}, bf16[2,8,512,128]{3,2,1,0:T(8,128)(2,1)S(1)}, u32[]{:S(2)}) copy-start(bf16[2,8,512,128]{3,2,1,0:T(8,128)(2,1)S(1)} %get-tuple-element.4.src) | copy-start | bytes 6291460

commit v2 on v1

--- a/solution.py
+++ b/solution.py
@@ -44,8 +44,8 @@
     lax.fori_loop(0, 8, tile, 0)
 
 
-def pool_body(ids, cnt, tab_hbm, out, offs, tab, ka, kb, iota, w, stage, sb, lv, lvall, tot, ztot, yline,
-              tsem, ssem, rsem, lsem, lss, lrs, zss, zrs, yss, yrs):
+def pool_body(ids_hbm, cnt_hbm, tab_hbm, out, offs, ids, cnt, tab, ka, kb, iota, w, stage, sb, lv, lvall, tot, ytot, ztot,
+              isem, tsem, ssem, rsem, lsem, lss, lrs, zss, zrs, yss, yrs):
     b, k = lax.axis_index("batch"), lax.axis_index("table")
     y, z = b // NZ, b % NZ
     x, c = k // 2, k % 2
@@ -54,17 +54,25 @@
     for d in range(1, NK):
         pl.semaphore_signal(bar, inc=1, device_id=(b, (k + d) % NK), device_id_type=MESH)
     for d in range(1, NZ):
-        pl.semaphore_signal(bar, inc=1, device_id=(y * NZ + (z + d) % NZ, k), device_id_type=MESH)
+        @pl.when(z + d < NZ)
+        def _():
+            pl.semaphore_signal(bar, inc=1, device_id=(b + d, k), device_id_type=MESH)
     for d in range(1, NY):
         pl.semaphore_signal(bar, inc=1, device_id=(((y + d) % NY) * NZ + z, k), device_id_type=MESH)
 
     def table_copy(t):
         return pltpu.make_async_copy(tab_hbm.at[t], tab.at[t], tsem.at[t])
 
+    id_copy = pltpu.make_async_copy(ids_hbm, ids, isem.at[0])
+    count_copy = pltpu.make_async_copy(cnt_hbm, cnt, isem.at[1])
+    id_copy.start()
+    count_copy.start()
     for t in range(NT):
         table_copy(t).start()
 
     iota[...] = lax.broadcasted_iota(I32, (256, 256), 0).astype(F32).astype(BF)
+    id_copy.wait()
+    count_copy.wait()
     make_keys(ids, cnt, ka, kb)
 
     for q in range(8):
@@ -95,15 +103,25 @@
             src_ref=lv, dst_ref=lvall.at[k], send_sem=lss.at[d], recv_sem=lrs.at[k],
             device_id=(b, (k + d) % NK), device_id_type=MESH)
 
+    def y_copy(d):
+        return pltpu.make_async_remote_copy(
+            src_ref=tot, dst_ref=ytot.at[y], send_sem=yss.at[d], recv_sem=yrs.at[y],
+            device_id=(((y + d) % NY) * NZ + z, k), device_id_type=MESH)
+
     def z_copy(d):
         return pltpu.make_async_remote_copy(
-            src_ref=tot, dst_ref=ztot.at[z], send_sem=zss.at[d], recv_sem=zrs.at[z],
-            device_id=(y * NZ + (z + d) % NZ, k), device_id_type=MESH)
-
-    def y_copy(d):
-        return pltpu.make_async_remote_copy(
-            src_ref=yline.at[y], dst_ref=yline.at[y], send_sem=yss.at[d], recv_sem=yrs.at[y],
-            device_id=(((y + d) % NY) * NZ + z, k), device_id_type=MESH)
+            src_ref=ztot.at[z], dst_ref=ztot.at[z], send_sem=zss.at[d + NZ], recv_sem=zrs.at[z],
+            device_id=(b + d, k), device_id_type=MESH)
+
+    def z_arrival(d):
+        return arrival(ztot.at[z + d], zrs.at[z + d])
+
+    def reply(lo, hi):
+        for d in range(lo, hi):
+            @pl.when(z + d < NZ)
+            def _():
+                z_arrival(d).wait_recv()
+                z_copy(d).start()
 
     def arrival(ref, sem):
         return pltpu.make_async_remote_copy(
@@ -178,7 +196,7 @@
 
         @pl.when(i == 4)
         def _():
-            pl.semaphore_wait(bar, NK - 1 + NZ - 1 + NY - 1)
+            pl.semaphore_wait(bar, NK - 1 + NY - 1 + z)
             for d in range(1, NK):
                 live_copy(d).start()
 
@@ -186,25 +204,35 @@
         def _():
             finish(i // 4 - 1)
 
-        @pl.when(i == 9)
+        @pl.when(i == 8)
         def _():
             for d in range(1, NK):
                 arrival(lvall.at[(k + d) % NK], lrs.at[(k + d) % NK]).wait_recv()
             tot[...] = sum_all(pairs_of())
-            ztot[z] = tot[...]
-            for d in range(1, NZ):
-                z_copy(d).start()
-
-        @pl.when(i == 21)
-        def _():
-            for d in range(1, NZ):
-                arrival(ztot.at[(z + d) % NZ], zrs.at[(z + d) % NZ]).wait_recv()
-            line = ztot[0]
-            for d in range(1, NZ):
-                line = line + ztot[d]
-            yline[y] = line
             for d in range(1, NY):
                 y_copy(d).start()
+
+        @pl.when(i == 12)
+        def _():
+            for d in range(1, NY):
+                arrival(ytot.at[(y + d) % NY], yrs.at[(y + d) % NY]).wait_recv()
+            sub = lax.broadcasted_iota(I32, (8, LANES), 0)
+            col = jnp.where(sub == y, tot[...], 0)
+            for d in range(1, NY):
+                col = jnp.where(sub == (y + d) % NY, ytot[(y + d) % NY], col)
+            ztot[z] = col
+            for d in range(1, NZ):
+                @pl.when(z - d >= 0)
+                def _():
+                    z_copy(-d).start()
+
+        @pl.when(i == 20)
+        def _():
+            reply(1, 4)
+
+        @pl.when(i == 26)
+        def _():
+            reply(4, 8)
 
         return carry
 
@@ -213,15 +241,18 @@
     second(31, 1)
     finish(7)
 
-    for d in range(1, NY):
-        arrival(yline.at[(y + d) % NY], yrs.at[(y + d) % NY]).wait_recv()
+    reply(8, NZ)
+    for d in range(1, NZ):
+        @pl.when(z - d >= 0)
+        def _():
+            z_arrival(-d).wait_recv()
     lane = lax.broadcasted_iota(I32, (8, LANES), 1)
     sub = lax.broadcasted_iota(I32, (8, LANES), 0)
     before = jnp.zeros((8, LANES), I32)
-    for d in range(NY):
-        before = before + jnp.where(d < y, yline[d], 0)
-    for d in range(NZ):
-        before = before + jnp.where(d < z, ztot[d], 0)
+    for n in range(NZ):
+        earlier = jnp.logical_or(sub < y, jnp.logical_and(sub == y, n < z))
+        before = before + jnp.where(earlier, ztot[n], 0)
+    before = jnp.broadcast_to(jnp.sum(before, axis=0, keepdims=True), (8, LANES))
     pairs = pairs_of()
     run = pairs
     for n in range(7):
@@ -233,7 +264,13 @@
     for d in range(1, NK):
         live_copy(d).wait_send()
     for d in range(1, NZ):
-        z_copy(d).wait_send()
+        @pl.when(z + d < NZ)
+        def _():
+            z_copy(d).wait_send()
+
+        @pl.when(z - d >= 0)
+        def _():
+            z_copy(-d).wait_send()
     for d in range(1, NY):
         y_copy(d).wait_send()
     for h in range(2):
@@ -252,9 +289,11 @@
     return pl.pallas_call(
         pool_body,
         out_shape=(jax.ShapeDtypeStruct((2, NK, 512, LANES), BF), jax.ShapeDtypeStruct((1, LANES), I32)),
-        in_specs=[pl.BlockSpec(memory_space=pltpu.VMEM)] * 2 + [pl.BlockSpec(memory_space=pl.ANY)],
-        out_specs=(pl.BlockSpec(memory_space=pl.ANY), pl.BlockSpec(memory_space=pltpu.VMEM)),
+        in_specs=[pl.BlockSpec(memory_space=pltpu.HBM)] * 3,
+        out_specs=(pl.BlockSpec(memory_space=pltpu.HBM), pl.BlockSpec(memory_space=pltpu.VMEM)),
         scratch_shapes=[
+            pltpu.VMEM((64, 1024), I32),
+            pltpu.VMEM((NT, 1024), I32),
             pltpu.VMEM((NT, 2048, LANES), BF),
             pltpu.VMEM((8, NT, 4, 256), F32),
             pltpu.VMEM((8, NT, 4, 256), F32),
@@ -265,13 +304,13 @@
             pltpu.VMEM((8, LANES), I32),
             pltpu.VMEM((NK, 8, LANES), I32),
             pltpu.VMEM((8, LANES), I32),
+            pltpu.VMEM((NY, 8, LANES), I32),
             pltpu.VMEM((NZ, 8, LANES), I32),
-            pltpu.VMEM((NY, 8, LANES), I32),
-            dma((NT,)), dma((16,)), dma((16,)), dma((2,)),
-            dma((NK,)), dma((NK,)), dma((NZ,)), dma((NZ,)), dma((NY,)), dma((NY,)),
+            dma((2,)), dma((NT,)), dma((16,)), dma((16,)), dma((2,)),
+            dma((NK,)), dma((NK,)), dma((2 * NZ,)), dma((NZ,)), dma((NY,)), dma((NY,)),
         ],
         compiler_params=pltpu.CompilerParams(
-            collective_id=0, has_side_effects=True, vmem_limit_bytes=40 * 2**20),
+            collective_id=0, has_side_effects=True, vmem_limit_bytes=60 * 2**20),
         name="pool_exchange",
     )(ids, cnt, tab)
 

time: 58.3 us -> 52.3 us (0.90)
  local copies, waits for them, and re-layouts: 5.72 us -> 1.14 us
  Pallas kernels: 51.7 us -> 50.3 us
    unnamed x9 -> x1, local copies, waits for them, and re-layouts: 5.72 us -> 1.14 us
    pallas_call x1, Pallas kernels: 45.2 us -> 43.8 us  [pool_exchange(): pl.pallas_call(pool_body, out_shape=(jax.ShapeDtypeStruct((2, NK, 512, LA...]
where the time goes in v2:
time: 52.3 us; the launch traced here: 52.1 us
  Pallas kernels  50.3 us (96%)
  local copies, waits for them, and re-layouts  1.14 us (2%)
  between operations  0.64 us (1%)
    pallas_call x1, Pallas kernels, pool_exchange(): pl.pallas_call(pool_body, out_shape=(jax.ShapeDtypeStruct((2, NK, 512, LA...  43.8 us
    pallas_call x1, Pallas kernels, gram(): pl.pallas_call(gram_body, grid=(4,), out_shape=jax.ShapeDtypeStruct((128,...  6.46 us
    unnamed x1, local copies, waits for them, and re-layouts  1.14 us

profile of v2, /device:TPU:1, one launch (start us, length us, event | category | flops | bytes accessed | tf_op | source)
XLA Modules:
  0.0 52.1 jit_solution(283285304895361673)
XLA Ops:
  0.6 43.8 %pool_exchange.1 = (bf16[2,8,512,128]{3,2,1,0:T(8,128)(2,1)}, s32[1,128]{1,0:T(1,128)}) custom-call(s32[64,1024]{1,0:T(8,128)} %bitcast.3, s32[8,1024]{1,0:T(8,128)} %bitcast.4, bf16[8,2048,128]{2,1,0:T(8,128)(2,1)} %tab_hbm.1), custom_call_target="tpu_custom_call" | custom-call | tf_op jit(solution)/shard_map/pool_exchange/pallas_call | solution.py:289
  44.5 6.5 %gram.1 = bf16[128,4096]{1,0:T(8,128)(2,1)} custom-call(bf16[2,8,512,128]{3,2,1,0:T(8,128)(2,1)} %get-tuple-element.4.src), custom_call_target="tpu_custom_call" | custom-call | tf_op jit(solution)/shard_map/gram/pallas_call | solution.py:337
  50.9 1.1 %copy.6 = s32[128]{0:T(128)} copy(s32[128]{0:T(128)} %bitcast.5) | data formatting | bytes 1024

commit v3 on v2

--- a/solution.py
+++ b/solution.py
@@ -17,34 +17,7 @@
 TRI = (((1,), (1,)), ((), ()))
 
 
-def make_keys(ids, cnt, ka, kb):
-    lane = lax.broadcasted_iota(I32, (8, LANES), 1)
-    sub = lax.broadcasted_iota(I32, (8, LANES), 0)
-    place = [jnp.logical_and((sub & 3) == b, (lane >> 5) == b) for b in range(4)]
-
-    def tile(q, carry):
-        c0 = pl.multiple_of(q * LANES, LANES)
-        for t in range(NT):
-            v = ids[t * 8 : t * 8 + 8, pl.ds(c0, LANES)]
-            v = jnp.where(sub >= cnt[t : t + 1, pl.ds(c0, LANES)], 2048, v)
-            turned = [v] + [pltpu.roll(v, 32 * k, 1) for k in range(1, 4)]
-            for a in range(4):
-                m = jnp.zeros_like(v)
-                for b in range(4):
-                    m = jnp.where(place[b], turned[(b - a) % 4], m)
-                m = m + pltpu.roll(m, 7, 0)
-                m = m + pltpu.roll(m, 6, 0)
-                za = (((m >> 8) << 5) + (lane & 31)).astype(F32)
-                zb = (m & 255).astype(F32)
-                for h in range(2):
-                    ka[q, t, a : a + 1, h * 128 : h * 128 + 128] = za[4 * h : 4 * h + 1, :]
-                    kb[q, t, a : a + 1, h * 128 : h * 128 + 128] = zb[4 * h : 4 * h + 1, :]
-        return carry
-
-    lax.fori_loop(0, 8, tile, 0)
-
-
-def pool_body(ids_hbm, cnt_hbm, tab_hbm, out, offs, ids, cnt, tab, ka, kb, iota, w, stage, sb, lv, lvall, tot, ytot, ztot,
+def pool_body(ids_hbm, cnt_hbm, tab_hbm, out, offs, ids, cnt, cntb, tab, ka, kb, iota, w, stage, sb, lv, lvall, tot, ytot, ztot,
               isem, tsem, ssem, rsem, lsem, lss, lrs, zss, zrs, yss, yrs):
     b, k = lax.axis_index("batch"), lax.axis_index("table")
     y, z = b // NZ, b % NZ
@@ -73,7 +46,8 @@
     iota[...] = lax.broadcasted_iota(I32, (256, 256), 0).astype(F32).astype(BF)
     id_copy.wait()
     count_copy.wait()
-    make_keys(ids, cnt, ka, kb)
+    for t in range(NT):
+        cntb[t] = jnp.broadcast_to(cnt[t : t + 1, :], (8, 1024))
 
     for q in range(8):
         on = (cnt[:, q * 128 : q * 128 + 128] > 0).astype(I32)
@@ -131,14 +105,38 @@
         j = i // 4
         return j, j // 4, (x + turn(j % 4)) % 4, (i % 4) * 2
 
+    lane = lax.broadcasted_iota(I32, (8, LANES), 1)
+    sub = lax.broadcasted_iota(I32, (8, LANES), 0)
+    place = [jnp.logical_and((sub & 3) == n, (lane >> 5) == n) for n in range(4)]
+
+    def keys(i, slot):
+        j, h, xd, t0 = rows_of(i)
+        for tt in range(2):
+            for qq in range(2):
+                c0 = pl.multiple_of((xd * 2 + qq) * LANES, LANES)
+                v = ids[pl.ds(pl.multiple_of((t0 + tt) * 8, 8), 8), pl.ds(c0, LANES)]
+                v = jnp.where(sub >= cntb[t0 + tt, :, pl.ds(c0, LANES)], 2048, v)
+                v = jnp.where(h > 0, pltpu.roll(v, 64, 1), v)
+                turned = [v] + [pltpu.roll(v, 32 * n, 1) for n in range(1, 4)]
+                for a in range(2):
+                    m = jnp.zeros_like(v)
+                    for n in range(4):
+                        m = jnp.where(place[n], turned[(n - a) % 4], m)
+                    m = m + pltpu.roll(m, 7, 0)
+                    m = m + pltpu.roll(m, 6, 0)
+                    za = (((m >> 8) << 5) + (lane & 31)).astype(F32)
+                    zb = (m & 255).astype(F32)
+                    g = qq * 2 + a
+                    for n in range(2):
+                        ka[slot, tt, g : g + 1, n * 128 : n * 128 + 128] = za[4 * n : 4 * n + 1, :]
+                        kb[slot, tt, g : g + 1, n * 128 : n * 128 + 128] = zb[4 * n : 4 * n + 1, :]
+
     def first(i, slot):
-        j, h, xd, t0 = rows_of(i)
         one, zero = jnp.ones((16, 256), BF), jnp.zeros((16, 256), BF)
         for tt in range(2):
             for g in range(4):
-                q, a = xd * 2 + g // 2, h * 2 + g % 2
-                ra = jnp.broadcast_to(ka[q, t0 + tt, pl.ds(a, 1), :], (16, 256)).astype(BF)
-                rb = jnp.broadcast_to(kb[q, t0 + tt, pl.ds(a, 1), :], (16, 256)).astype(BF)
+                ra = jnp.broadcast_to(ka[slot, tt, g : g + 1, :], (16, 256)).astype(BF)
+                rb = jnp.broadcast_to(kb[slot, tt, g : g + 1, :], (16, 256)).astype(BF)
                 la, lb = [], []
                 for r in range(16):
                     row = iota[r * 16 : r * 16 + 16, :]
@@ -183,28 +181,32 @@
         s = jnp.sum(jnp.sum(v, axis=0, keepdims=True), axis=1, keepdims=True)
         return jnp.broadcast_to(s, (8, LANES))
 
-    def step(i, carry):
-        slot = i % 2
-
-        @pl.when(i <= 4)
-        def _():
-            table_copy((i - 1) * 2).wait()
-            table_copy((i - 1) * 2 + 1).wait()
-
-        second(i - 1, 1 - slot)
-        first(i, slot)
-
-        @pl.when(i == 4)
+    def step(p, carry):
+        i = 2 * p + 1
+
+        @pl.when(p < 2)
+        def _():
+            for n in range(4):
+                table_copy(p * 4 + n).wait()
+
+        second(i - 1, 0)
+        first(i, 1)
+        keys(i + 1, 0)
+        second(i, 1)
+        first(i + 1, 0)
+        keys(i + 2, 1)
+
+        @pl.when(p == 0)
         def _():
             pl.semaphore_wait(bar, NK - 1 + NY - 1 + z)
             for d in range(1, NK):
                 live_copy(d).start()
 
-        @pl.when(i % 4 == 0)
-        def _():
-            finish(i // 4 - 1)
-
-        @pl.when(i == 8)
+        @pl.when(p % 2 == 1)
+        def _():
+            finish(p // 2)
+
+        @pl.when(p == 2)
         def _():
             for d in range(1, NK):
                 arrival(lvall.at[(k + d) % NK], lrs.at[(k + d) % NK]).wait_recv()
@@ -212,11 +214,10 @@
             for d in range(1, NY):
                 y_copy(d).start()
 
-        @pl.when(i == 12)
+        @pl.when(p == 3)
         def _():
             for d in range(1, NY):
                 arrival(ytot.at[(y + d) % NY], yrs.at[(y + d) % NY]).wait_recv()
-            sub = lax.broadcasted_iota(I32, (8, LANES), 0)
             col = jnp.where(sub == y, tot[...], 0)
             for d in range(1, NY):
                 col = jnp.where(sub == (y + d) % NY, ytot[(y + d) % NY], col)
@@ -226,18 +227,22 @@
                 def _():
                     z_copy(-d).start()
 
-        @pl.when(i == 20)
+        @pl.when(p == 8)
         def _():
             reply(1, 4)
 
-        @pl.when(i == 26)
+        @pl.when(p == 11)
         def _():
             reply(4, 8)
 
         return carry
 
+    keys(0, 0)
     first(0, 0)
-    lax.fori_loop(1, 32, step, 0)
+    keys(1, 1)
+    lax.fori_loop(0, 15, step, 0)
+    second(30, 0)
+    first(31, 1)
     second(31, 1)
     finish(7)
 
@@ -246,8 +251,6 @@
         @pl.when(z - d >= 0)
         def _():
             z_arrival(-d).wait_recv()
-    lane = lax.broadcasted_iota(I32, (8, LANES), 1)
-    sub = lax.broadcasted_iota(I32, (8, LANES), 0)
     before = jnp.zeros((8, LANES), I32)
     for n in range(NZ):
         earlier = jnp.logical_or(sub < y, jnp.logical_and(sub == y, n < z))
@@ -294,9 +297,10 @@
         scratch_shapes=[
             pltpu.VMEM((64, 1024), I32),
             pltpu.VMEM((NT, 1024), I32),
+            pltpu.VMEM((NT, 8, 1024), I32),
             pltpu.VMEM((NT, 2048, LANES), BF),
-            pltpu.VMEM((8, NT, 4, 256), F32),
-            pltpu.VMEM((8, NT, 4, 256), F32),
+            pltpu.VMEM((2, 2, 4, 256), F32),
+            pltpu.VMEM((2, 2, 4, 256), F32),
             pltpu.VMEM((256, 256), BF),
             pltpu.VMEM((2, 2, 8, 128, 256), BF),
             pltpu.VMEM((1024, LANES), F32),
@@ -315,32 +319,38 @@
     )(ids, cnt, tab)
 
 
+PITCH = 72
+
+
 def gram_body(src, out, g):
-    low = lax.broadcasted_iota(I32, (16, LANES), 1) < 64
-    for half in range(2):
-        for p in range(8):
-            r0 = half * 128 + p * 16
-            got = [src[0, s, r0 : r0 + 16, :].astype(F32) for s in range(NK)]
-            even = jnp.concatenate([v[0:8] for v in got], 0).astype(BF)
-            odd = jnp.concatenate([v[8:16] for v in got], 0).astype(BF)
-            for n, m in ((0, even), (1, odd)):
-                full = lax.dot_general(m, jnp.concatenate([m, m], 0), TRI, preferred_element_type=F32)
-                g[half, (p * 2 + n) * 64 : (p * 2 + n) * 64 + 64, :] = full
-    for half in range(2):
-        for i in range(32):
-            lo = g[half, pl.ds(2 * i, 16, 64), :]
-            hi = g[half, pl.ds(2 * i + 1, 16, 64), :]
-            out[half * 16 : half * 16 + 16, i * 128 : i * 128 + 128] = jnp.where(low, lo, hi).astype(BF)
+    low = lax.broadcasted_iota(I32, (64, LANES), 1) < 64
+    low8 = low[0:8]
+    got = [src[0, n].astype(F32) for n in range(NK)]
+
+    def vectors(m):
+        return jnp.concatenate([v[m * 8 : m * 8 + 8] for v in got], 0)
+
+    for m in (0, 2, 4, 6):
+        four = jnp.concatenate([vectors(n) for n in (m, m + 8, m + 1, m + 9)], 0).astype(BF)
+        full = lax.dot_general(four, four, TRI, preferred_element_type=F32)
+        g[m * PITCH : m * PITCH + 64, :] = jnp.where(low, full[0:64, 0:128], full[64:128, 0:128])
+        g[(m + 1) * PITCH : (m + 1) * PITCH + 64, :] = jnp.where(low, full[128:192, 128:], full[192:256, 128:])
+    for i in range(32):
+        even = g[pl.ds(2 * i, 8, PITCH), :]
+        odd = g[pl.ds(2 * i + 1, 8, PITCH), :]
+        a = jnp.where(low8, even, pltpu.roll(odd, 64, 1))
+        b = jnp.where(low8, pltpu.roll(even, 64, 1), odd)
+        out[:, i * 128 : i * 128 + 128] = jnp.concatenate([a, b], 0).astype(BF)
 
 
 def gram(got):
     return pl.pallas_call(
         gram_body,
-        grid=(4,),
+        grid=(8,),
         out_shape=jax.ShapeDtypeStruct((128, 4096), BF),
-        in_specs=[pl.BlockSpec((1, NK, 256, LANES), lambda i: (i // 2, 0, i % 2, 0))],
-        out_specs=pl.BlockSpec((32, 4096), lambda i: (i, 0)),
-        scratch_shapes=[pltpu.VMEM((2, 1024, LANES), F32)],
+        in_specs=[pl.BlockSpec((1, NK, 128, LANES), lambda i: (i // 4, 0, i % 4, 0))],
+        out_specs=pl.BlockSpec((16, 4096), lambda i: (i, 0)),
+        scratch_shapes=[pltpu.VMEM((8 * PITCH, LANES), F32)],
         name="gram",
     )(got)
 

time: 52.3 us -> 49.9 us (0.954)
  Pallas kernels: 50.3 us -> 47.8 us
    pallas_call x1, Pallas kernels: 43.8 us -> 40.9 us  [pool_exchange(): pl.pallas_call(pool_body, out_shape=(jax.ShapeDtypeStruct((2, NK, 512, LA...]
where the time goes in v3:
time: 49.9 us; the launch traced here: 49.6 us
  Pallas kernels  47.8 us (96%)
  local copies, waits for them, and re-layouts  1.14 us (2%)
  between operations  0.64 us (1%)
    pallas_call x1, Pallas kernels, pool_exchange(): pl.pallas_call(pool_body, out_shape=(jax.ShapeDtypeStruct((2, NK, 512, LA...  40.9 us
    pallas_call x1, Pallas kernels, gram(): pl.pallas_call(gram_body, grid=(8,), out_shape=jax.ShapeDtypeStruct((128,...  6.92 us
    unnamed x1, local copies, waits for them, and re-layouts  1.14 us

profile of v3, /device:TPU:1, one launch (start us, length us, event | category | flops | bytes accessed | tf_op | source)
XLA Modules:
  0.0 49.6 jit_solution(8779789069996698426)
XLA Ops:
  0.6 40.9 %pool_exchange.1 = (bf16[2,8,512,128]{3,2,1,0:T(8,128)(2,1)}, s32[1,128]{1,0:T(1,128)}) custom-call(s32[64,1024]{1,0:T(8,128)} %bitcast.3, s32[8,1024]{1,0:T(8,128)} %bitcast.4, bf16[8,2048,128]{2,1,0:T(8,128)(2,1)} %tab_hbm.1), custom_call_target="tpu_custom_call" | custom-call | tf_op jit(solution)/shard_map/pool_exchange/pallas_call | solution.py:292
  41.6 6.9 %gram.1 = bf16[128,4096]{1,0:T(8,128)(2,1)} custom-call(bf16[2,8,512,128]{3,2,1,0:T(8,128)(2,1)} %get-tuple-element.4.src), custom_call_target="tpu_custom_call" | custom-call | tf_op jit(solution)/shard_map/gram/pallas_call | solution.py:347
  48.5 1.1 %copy.6 = s32[128]{0:T(128)} copy(s32[128]{0:T(128)} %bitcast.5) | data formatting | bytes 1024

commit v4 on v3

--- a/solution.py
+++ b/solution.py
@@ -14,6 +14,7 @@
 NK = 8
 NY, NZ = 4, 16
 LANES = 128
+RANK = (0, 1, 2, 3, 4, 5, 6, 7, 8, 10, 12, 14, 15, 13, 11, 9)
 TRI = (((1,), (1,)), ((), ()))
 
 
@@ -22,14 +23,15 @@
     b, k = lax.axis_index("batch"), lax.axis_index("table")
     y, z = b // NZ, b % NZ
     x, c = k // 2, k % 2
+    rank = sum(r * (1 - ((z - n) * (z - n) + 255) // 256) for n, r in enumerate(RANK))
 
     bar = pltpu.get_barrier_semaphore()
     for d in range(1, NK):
         pl.semaphore_signal(bar, inc=1, device_id=(b, (k + d) % NK), device_id_type=MESH)
-    for d in range(1, NZ):
-        @pl.when(z + d < NZ)
-        def _():
-            pl.semaphore_signal(bar, inc=1, device_id=(b + d, k), device_id_type=MESH)
+    for n in range(NZ):
+        @pl.when(RANK[n] > rank)
+        def _():
+            pl.semaphore_signal(bar, inc=1, device_id=(y * NZ + n, k), device_id_type=MESH)
     for d in range(1, NY):
         pl.semaphore_signal(bar, inc=1, device_id=(((y + d) % NY) * NZ + z, k), device_id_type=MESH)
 
@@ -82,20 +84,20 @@
             src_ref=tot, dst_ref=ytot.at[y], send_sem=yss.at[d], recv_sem=yrs.at[y],
             device_id=(((y + d) % NY) * NZ + z, k), device_id_type=MESH)
 
-    def z_copy(d):
-        return pltpu.make_async_remote_copy(
-            src_ref=ztot.at[z], dst_ref=ztot.at[z], send_sem=zss.at[d + NZ], recv_sem=zrs.at[z],
-            device_id=(b + d, k), device_id_type=MESH)
-
-    def z_arrival(d):
-        return arrival(ztot.at[z + d], zrs.at[z + d])
+    def z_copy(n):
+        return pltpu.make_async_remote_copy(
+            src_ref=ztot.at[z], dst_ref=ztot.at[z], send_sem=zss.at[n], recv_sem=zrs.at[z],
+            device_id=(y * NZ + n, k), device_id_type=MESH)
+
+    def z_arrival(n):
+        return arrival(ztot.at[n], zrs.at[n])
 
     def reply(lo, hi):
-        for d in range(lo, hi):
-            @pl.when(z + d < NZ)
+        for n in range(NZ):
+            @pl.when(jnp.logical_and(RANK[n] - rank >= lo, RANK[n] - rank < hi))
             def _():
-                z_arrival(d).wait_recv()
-                z_copy(d).start()
+                z_arrival(n).wait_recv()
+                z_copy(n).start()
 
     def arrival(ref, sem):
         return pltpu.make_async_remote_copy(
@@ -198,7 +200,7 @@
 
         @pl.when(p == 0)
         def _():
-            pl.semaphore_wait(bar, NK - 1 + NY - 1 + z)
+            pl.semaphore_wait(bar, NK - 1 + NY - 1 + rank)
             for d in range(1, NK):
                 live_copy(d).start()
 
@@ -222,10 +224,10 @@
             for d in range(1, NY):
                 col = jnp.where(sub == (y + d) % NY, ytot[(y + d) % NY], col)
             ztot[z] = col
-            for d in range(1, NZ):
-                @pl.when(z - d >= 0)
+            for n in range(NZ):
+                @pl.when(RANK[n] < rank)
                 def _():
-                    z_copy(-d).start()
+                    z_copy(n).start()
 
         @pl.when(p == 8)
         def _():
@@ -247,10 +249,10 @@
     finish(7)
 
     reply(8, NZ)
-    for d in range(1, NZ):
-        @pl.when(z - d >= 0)
-        def _():
-            z_arrival(-d).wait_recv()
+    for n in range(NZ):
+        @pl.when(RANK[n] < rank)
+        def _():
+            z_arrival(n).wait_recv()
     before = jnp.zeros((8, LANES), I32)
     for n in range(NZ):
         earlier = jnp.logical_or(sub < y, jnp.logical_and(sub == y, n < z))
@@ -266,14 +268,10 @@
 
     for d in range(1, NK):
         live_copy(d).wait_send()
-    for d in range(1, NZ):
-        @pl.when(z + d < NZ)
-        def _():
-            z_copy(d).wait_send()
-
-        @pl.when(z - d >= 0)
-        def _():
-            z_copy(-d).wait_send()
+    for n in range(NZ):
+        @pl.when(RANK[n] != rank)
+        def _():
+            z_copy(n).wait_send()
     for d in range(1, NY):
         y_copy(d).wait_send()
     for h in range(2):
@@ -311,7 +309,7 @@
             pltpu.VMEM((NY, 8, LANES), I32),
             pltpu.VMEM((NZ, 8, LANES), I32),
             dma((2,)), dma((NT,)), dma((16,)), dma((16,)), dma((2,)),
-            dma((NK,)), dma((NK,)), dma((2 * NZ,)), dma((NZ,)), dma((NY,)), dma((NY,)),
+            dma((NK,)), dma((NK,)), dma((NZ,)), dma((NZ,)), dma((NY,)), dma((NY,)),
         ],
         compiler_params=pltpu.CompilerParams(
             collective_id=0, has_side_effects=True, vmem_limit_bytes=60 * 2**20),
@@ -322,35 +320,63 @@
 PITCH = 72
 
 
-def gram_body(src, out, g):
+def gram_body(src, out, buf, res, g, isem, osem):
     low = lax.broadcasted_iota(I32, (64, LANES), 1) < 64
     low8 = low[0:8]
-    got = [src[0, n].astype(F32) for n in range(NK)]
-
-    def vectors(m):
-        return jnp.concatenate([v[m * 8 : m * 8 + 8] for v in got], 0)
-
-    for m in (0, 2, 4, 6):
-        four = jnp.concatenate([vectors(n) for n in (m, m + 8, m + 1, m + 9)], 0).astype(BF)
-        full = lax.dot_general(four, four, TRI, preferred_element_type=F32)
-        g[m * PITCH : m * PITCH + 64, :] = jnp.where(low, full[0:64, 0:128], full[64:128, 0:128])
-        g[(m + 1) * PITCH : (m + 1) * PITCH + 64, :] = jnp.where(low, full[128:192, 128:], full[192:256, 128:])
-    for i in range(32):
-        even = g[pl.ds(2 * i, 8, PITCH), :]
-        odd = g[pl.ds(2 * i + 1, 8, PITCH), :]
-        a = jnp.where(low8, even, pltpu.roll(odd, 64, 1))
-        b = jnp.where(low8, pltpu.roll(even, 64, 1), odd)
-        out[:, i * 128 : i * 128 + 128] = jnp.concatenate([a, b], 0).astype(BF)
+
+    def load(n):
+        return pltpu.make_async_copy(
+            src.at[n // 2, :, pl.ds(pl.multiple_of((n % 2) * 256, 256), 256)], buf.at[n], isem.at[n])
+
+    def store(n):
+        return pltpu.make_async_copy(
+            res.at[n], out.at[pl.ds(pl.multiple_of(n * 32, 32), 32)], osem.at[n])
+
+    for n in range(4):
+        load(n).start()
+
+    def part(n, carry):
+        load(n).wait()
+        for half in range(2):
+            got = [buf[n, v, half * 128 : half * 128 + 128].astype(F32) for v in range(NK)]
+
+            def vectors(m):
+                return jnp.concatenate([v[m * 8 : m * 8 + 8] for v in got], 0)
+
+            for m in (0, 2, 4, 6):
+                four = jnp.concatenate([vectors(r) for r in (m, m + 8, m + 1, m + 9)], 0).astype(BF)
+                full = lax.dot_general(four, four, TRI, preferred_element_type=F32)
+                g[half, m * PITCH : m * PITCH + 64, :] = jnp.where(low, full[0:64, 0:128], full[64:128, 0:128])
+                g[half, (m + 1) * PITCH : (m + 1) * PITCH + 64, :] = jnp.where(
+                    low, full[128:192, 128:], full[192:256, 128:])
+        for half in range(2):
+            for i in range(32):
+                even = g[half, pl.ds(2 * i, 8, PITCH), :]
+                odd = g[half, pl.ds(2 * i + 1, 8, PITCH), :]
+                a = jnp.where(low8, even, pltpu.roll(odd, 64, 1))
+                b = jnp.where(low8, pltpu.roll(even, 64, 1), odd)
+                res[n, half * 16 : half * 16 + 16, i * 128 : i * 128 + 128] = jnp.concatenate([a, b], 0).astype(BF)
+        store(n).start()
+        return carry
+
+    lax.fori_loop(0, 4, part, 0)
+    for n in range(4):
+        store(n).wait()
 
 
 def gram(got):
     return pl.pallas_call(
         gram_body,
-        grid=(8,),
         out_shape=jax.ShapeDtypeStruct((128, 4096), BF),
-        in_specs=[pl.BlockSpec((1, NK, 128, LANES), lambda i: (i // 4, 0, i % 4, 0))],
-        out_specs=pl.BlockSpec((16, 4096), lambda i: (i, 0)),
-        scratch_shapes=[pltpu.VMEM((8 * PITCH, LANES), F32)],
+        in_specs=[pl.BlockSpec(memory_space=pltpu.HBM)],
+        out_specs=pl.BlockSpec(memory_space=pltpu.HBM),
+        scratch_shapes=[
+            pltpu.VMEM((4, NK, 256, LANES), BF),
+            pltpu.VMEM((4, 32, 4096), BF),
+            pltpu.VMEM((2, 8 * PITCH, LANES), F32),
+            pltpu.SemaphoreType.DMA((4,)),
+            pltpu.SemaphoreType.DMA((4,)),
+        ],
         name="gram",
     )(got)
 

time: 49.9 us -> 47.3 us (0.948); the launches traced: 49.6 us -> 46.4 us
  Pallas kernels: 47.8 us -> 44.6 us
    pallas_call x1, Pallas kernels: 6.92 us -> 3.99 us  [gram(): pl.pallas_call(gram_body, out_shape=jax.ShapeDtypeStruct((128, 4096), BF)...]
where the time goes in v4:
time: 47.3 us; the launch traced here: 46.4 us
  Pallas kernels  44.6 us (94%)
  local copies, waits for them, and re-layouts  1.14 us (2%)
  between operations  0.65 us (1%)
    pallas_call x1, Pallas kernels, pool_exchange(): pl.pallas_call(pool_body, out_shape=(jax.ShapeDtypeStruct((2, NK, 512, LA...  40.6 us
    pallas_call x1, Pallas kernels, gram(): pl.pallas_call(gram_body, out_shape=jax.ShapeDtypeStruct((128, 4096), BF)...  3.99 us
    unnamed x1, local copies, waits for them, and re-layouts  1.14 us

profile of v4, /device:TPU:1, one launch (start us, length us, event | category | flops | bytes accessed | tf_op | source)
XLA Modules:
  0.0 46.4 jit_solution(8576749859592320850)
XLA Ops:
  0.6 40.6 %pool_exchange.1 = (bf16[2,8,512,128]{3,2,1,0:T(8,128)(2,1)}, s32[1,128]{1,0:T(1,128)}) custom-call(s32[64,1024]{1,0:T(8,128)} %bitcast.3, s32[8,1024]{1,0:T(8,128)} %bitcast.4, bf16[8,2048,128]{2,1,0:T(8,128)(2,1)} %tab_hbm.1), custom_call_target="tpu_custom_call" | custom-call | tf_op jit(solution)/shard_map/pool_exchange/pallas_call | solution.py:290
  41.3 4.0 %gram.1 = bf16[128,4096]{1,0:T(8,128)(2,1)} custom-call(bf16[2,8,512,128]{3,2,1,0:T(8,128)(2,1)} %get-tuple-element.4.src), custom_call_target="tpu_custom_call" | custom-call | tf_op jit(solution)/shard_map/gram/pallas_call | solution.py:368
  45.3 1.1 %copy.6 = s32[128]{0:T(128)} copy(s32[128]{0:T(128)} %bitcast.5) | data formatting | bytes 1024

commit v5 on v4

--- a/solution.py
+++ b/solution.py
@@ -6,6 +6,7 @@
 from jax.sharding import PartitionSpec as P
 
 BF = jnp.bfloat16
+F8 = jnp.float8_e4m3fn
 F32 = jnp.float32
 I32 = jnp.int32
 MESH = pl.DeviceIdType.MESH
@@ -14,7 +15,7 @@
 NK = 8
 NY, NZ = 4, 16
 LANES = 128
-RANK = (0, 1, 2, 3, 4, 5, 6, 7, 8, 10, 12, 14, 15, 13, 11, 9)
+RANK = (0, 1, 2, 3, 4, 5, 6, 7, 8, 10, 12, 15, 14, 13, 11, 9)
 TRI = (((1,), (1,)), ((), ()))
 
 
@@ -144,7 +145,7 @@
                     row = iota[r * 16 : r * 16 + 16, :]
                     la.append(jnp.where(row == ra, one, zero))
                     lb.append(jnp.where(row == rb, one, zero))
-                n = lax.dot_general(jnp.concatenate(la, 0), jnp.concatenate(lb, 0), TRI,
+                n = lax.dot_general(jnp.concatenate(la, 0).astype(F8), jnp.concatenate(lb, 0).astype(F8), TRI,
                                     preferred_element_type=F32).astype(BF)
                 for hi in range(8):
                     w[slot, tt, hi, g * 32 : g * 32 + 32, :] = n[hi * 32 : hi * 32 + 32, :]
@@ -198,7 +199,7 @@
         first(i + 1, 0)
         keys(i + 2, 1)
 
-        @pl.when(p == 0)
+        @pl.when(p == 1)
         def _():
             pl.semaphore_wait(bar, NK - 1 + NY - 1 + rank)
             for d in range(1, NK):
@@ -208,7 +209,7 @@
         def _():
             finish(p // 2)
 
-        @pl.when(p == 2)
+        @pl.when(p == 3)
         def _():
             for d in range(1, NK):
                 arrival(lvall.at[(k + d) % NK], lrs.at[(k + d) % NK]).wait_recv()
@@ -216,7 +217,7 @@
             for d in range(1, NY):
                 y_copy(d).start()
 
-        @pl.when(p == 3)
+        @pl.when(p == 4)
         def _():
             for d in range(1, NY):
                 arrival(ytot.at[(y + d) % NY], yrs.at[(y + d) % NY]).wait_recv()
@@ -229,11 +230,11 @@
                 def _():
                     z_copy(n).start()
 
-        @pl.when(p == 8)
+        @pl.when(p == 9)
         def _():
             reply(1, 4)
 
-        @pl.when(p == 11)
+        @pl.when(p == 12)
         def _():
             reply(4, 8)
 

time: 47.3 us -> 45.7 us (0.966); the launches traced: 46.4 us -> 45.5 us
  Pallas kernels: 44.6 us -> 43.8 us
    pallas_call x1, Pallas kernels: 40.6 us -> 39.8 us  [pool_exchange(): pl.pallas_call(pool_body, out_shape=(jax.ShapeDtypeStruct((2, NK, 512, LA...]
where the time goes in v5:
time: 45.7 us; the launch traced here: 45.5 us
  Pallas kernels  43.8 us (96%)
  local copies, waits for them, and re-layouts  1.14 us (2%)
  between operations  0.65 us (1%)
    pallas_call x1, Pallas kernels, pool_exchange(): pl.pallas_call(pool_body, out_shape=(jax.ShapeDtypeStruct((2, NK, 512, LA...  39.8 us
    pallas_call x1, Pallas kernels, gram(): pl.pallas_call(gram_body, out_shape=jax.ShapeDtypeStruct((128, 4096), BF)...  3.99 us
    unnamed x1, local copies, waits for them, and re-layouts  1.14 us

profile of v5, /device:TPU:1, one launch (start us, length us, event | category | flops | bytes accessed | tf_op | source)
XLA Modules:
  0.0 45.5 jit_solution(1454748392532215724)
XLA Ops:
  0.6 39.8 %pool_exchange.1 = (bf16[2,8,512,128]{3,2,1,0:T(8,128)(2,1)}, s32[1,128]{1,0:T(1,128)}) custom-call(s32[64,1024]{1,0:T(8,128)} %bitcast.3, s32[8,1024]{1,0:T(8,128)} %bitcast.4, bf16[8,2048,128]{2,1,0:T(8,128)(2,1)} %tab_hbm.1), custom_call_target="tpu_custom_call" | custom-call | tf_op jit(solution)/shard_map/pool_exchange/pallas_call | solution.py:291
  40.4 4.0 %gram.1 = bf16[128,4096]{1,0:T(8,128)(2,1)} custom-call(bf16[2,8,512,128]{3,2,1,0:T(8,128)(2,1)} %get-tuple-element.4.src), custom_call_target="tpu_custom_call" | custom-call | tf_op jit(solution)/shard_map/gram/pallas_call | solution.py:369
  44.4 1.1 %copy.6 = s32[128]{0:T(128)} copy(s32[128]{0:T(128)} %bitcast.5) | data formatting | bytes 1024
